TPU v7x, 256 devices: a whole 4x4x8 slice. The times are simulated.
256 devices in a mesh: seq: 4 (over y_hi, core), blk: 64 (over z, x, y_lo).
Axes of the slice: x: 4, y: 4 (y_hi: 2, y_lo: 2; y = y_hi * 2 + y_lo), z: 8, core: 2. Of those that a mesh axis runs over, the one named last changes fastest.
Arguments:
- kv_cache: bfloat16 [4, 2, 16, 4096, 1024], P(None, None, None, ('seq', 'blk')), may hold values from -18 to 18, as said below
- queries: bfloat16 [4, 128, 1024], P(None, 'blk'), may hold values from -400 to 400
- fresh_key_value: bfloat16 [4, 2, 128, 128], P(None, None, 'blk'), may hold values from -70 to 70
- lengths: int32 [16], replicated, may hold values from 1 to 4096, 49152 in all
Outputs:
- quant_cache: bfloat16 [4, 2, 128, 4096, 128], P(None, None, 'blk', 'seq')
- block_scale: float32 [4, 2, 128, 32], P(None, None, 'blk', 'seq')
- attended: bfloat16 [4, 128, 1024], P(None, 'blk')
Inputs may be any that keep to these rules, and one draw needn't show every extreme that they name: `kv_cache`: each entry is a random value times a factor drawn for its position and head. `lengths`: every sequence has at least one live position, and some sequence uses all 4096.
All inputs are finite; a program needn't handle non-finite values.
Results may differ from a plain program's by a relative error of at most 0.003.
The roundings to bfloat16 on the way count: a program that leaves them out, or rounds other values in their place, can miss the bound.
Values may be sent and summed in bfloat16 or wider, within the bound.
A program may use at most 64 MiB of HBM per device.

v0:
```python
import jax
import jax.numpy as jnp
from jax import lax
from jax.sharding import PartitionSpec as P

HEAD_DIM = 128
QUERY_GROUP = 8
BLOCK = 128


def gathered_once(shard, axis):
    leaves = jax.tree.leaves(shard)
    turns = sorted(range(len(leaves)), key=lambda k: -leaves[k].size)
    width = (1, *leaves[turns[0]].shape)[-1]
    lines = [
        jnp.pad(leaves[k].reshape(-1), (0, -leaves[k].size % width)).reshape(-1, width)
        for k in turns
    ]
    both, at, found = (lax.all_gather(jnp.concatenate(lines), axis), 0, {})
    for k, line in zip(turns, lines):
        piece = both[:, at : at + len(line)].reshape(len(both), -1)
        found[k] = piece[:, : leaves[k].size].reshape(-1, *leaves[k].shape)
        at += len(line)
    numbers = iter(range(len(leaves)))
    return jax.tree.map(lambda _: found[next(numbers)], shard)


def joined(value, axis, join):
    pieces = gathered_once(value, axis)
    head = jax.tree.map(lambda part: part[0], pieces)
    tail = jax.tree.map(lambda part: part[1:], pieces)
    subtotal, _ = lax.scan(lambda subtotal, piece: (join(subtotal, piece), None), head, tail)
    return subtotal


def blend(first_part, second_part):
    peak = jnp.maximum(first_part[0], second_part[0])
    left = jnp.exp(first_part[0] - peak)
    right = jnp.exp(second_part[0] - peak)
    return (
        peak,
        first_part[1] * left + second_part[1] * right,
        first_part[2] * left[..., None] + second_part[2] * right[..., None],
    )


def on_device(kv_cache, queries, fresh_key_value, lengths):
    layers, _, batch, local_rows, width = kv_cache.shape
    heads = width // HEAD_DIM
    blk_count = lax.axis_size("blk")
    blk_place = lax.axis_index("blk")
    pairs_here = heads * batch // blk_count
    seq_rows = local_rows * blk_count
    blocks_here = seq_rows // BLOCK
    arranged = kv_cache.reshape(layers, 2, batch, local_rows, heads, HEAD_DIM).transpose(
        0, 1, 4, 2, 3, 5
    )
    arranged = arranged.reshape(layers, 2, heads * batch, local_rows, HEAD_DIM)
    pair_start = blk_place * pairs_here
    moved = lax.all_to_all(arranged, "blk", split_axis=2, concat_axis=3, tiled=True)
    grouped = moved.reshape(layers, 2, pairs_here, blocks_here, BLOCK, HEAD_DIM)
    block_scale = (
        jnp.maximum(jnp.max(jnp.abs(grouped), axis=(4, 5)).astype(jnp.float32), 1.0) / 127.0
    )
    quant = (grouped.astype(jnp.float32) / block_scale[..., None, None]).astype(jnp.bfloat16)
    quant = quant.reshape(layers, 2, pairs_here, seq_rows, HEAD_DIM)
    seq_start = lax.axis_index("seq") * seq_rows
    pair_len = lax.dynamic_slice_in_dim(jnp.tile(lengths, heads), pair_start, pairs_here)
    positions = seq_start + jnp.arange(seq_rows, dtype=jnp.int32).reshape(blocks_here, BLOCK)
    valid = positions[None] < pair_len[:, None, None]
    inverse = 1.0 / jnp.sqrt(jnp.float32(HEAD_DIM))
    grouped_queries = queries.reshape(layers, pairs_here, QUERY_GROUP, HEAD_DIM)
    peaks = []
    totals = []
    sums = []
    for layer in range(layers):
        raw = jnp.einsum(
            "pgd,prd->pgr",
            grouped_queries[layer],
            quant[layer, 0],
            preferred_element_type=jnp.float32,
        )
        scores = (
            raw.reshape(pairs_here, QUERY_GROUP, blocks_here, BLOCK)
            * block_scale[layer, 0][:, None, :, None]
            * inverse
        )
        masked = jnp.where(valid[:, None], scores, -1e30)
        block_top = jnp.max(masked, axis=-1)
        weight = jnp.where(valid[:, None], jnp.exp(masked - block_top[..., None]), 0.0)
        block_total = jnp.sum(weight, axis=-1)
        rounded = (weight * block_scale[layer, 1][:, None, :, None]).astype(jnp.bfloat16)
        values = quant[layer, 1].reshape(pairs_here, blocks_here, BLOCK, HEAD_DIM)
        block_sum = jnp.einsum(
            "pgnt,pntd->pgnd", rounded, values, preferred_element_type=jnp.float32
        )
        local_top = jnp.max(block_top, axis=-1)
        scale_factor = jnp.exp(block_top - local_top[..., None])
        peaks.append(local_top)
        totals.append(jnp.sum(scale_factor * block_total, axis=-1))
        sums.append(jnp.sum(scale_factor[..., None] * block_sum, axis=2))
    peak = jnp.stack(peaks)
    total = jnp.stack(totals)
    weighted = jnp.stack(sums)
    peak, total, weighted = joined((peak, total, weighted), "seq", blend)
    own = (
        jnp.einsum(
            "lpgd,lpd->lpg",
            grouped_queries,
            fresh_key_value[:, 0],
            preferred_element_type=jnp.float32,
        )
        * inverse
    )
    top = jnp.maximum(peak, own)
    cache_w = jnp.exp(peak - top)
    own_w = jnp.exp(own - top)
    numer = (
        weighted * cache_w[..., None]
        + own_w[..., None] * fresh_key_value[:, 1].astype(jnp.float32)[:, :, None, :]
    )
    denom = total * cache_w + own_w
    attended = (
        (numer / denom[..., None])
        .reshape(layers, pairs_here, QUERY_GROUP * HEAD_DIM)
        .astype(jnp.bfloat16)
    )
    return (quant, block_scale, attended)


def solution(mesh):
    in_specs = (
        P(None, None, None, ("seq", "blk"), None),
        P(None, "blk", None),
        P(None, None, "blk", None),
        P(),
    )
    out_specs = (
        P(None, None, "blk", "seq", None),
        P(None, None, "blk", "seq"),
        P(None, "blk", None),
    )
    return jax.shard_map(
        on_device, mesh=mesh, in_specs=in_specs, out_specs=out_specs, check_vma=False
    )
```

profile of v0, /device:TPU:1, one launch (start us, length us, event | category | flops | bytes accessed | tf_op | source)
XLA Modules:
  0.0 148.3 jit_solution(6706500304532185207)
XLA Ops:
  0.6 3.3 %copy.33 = bf16[256,8,8,128]{3,2,1,0:T(8,128)(2,1)S(1)} copy(bf16[256,8,8,128]{3,1,2,0:T(8,128)(2,1)} %bitcast.273) | data formatting | bytes 8388608
  3.9 1.1 copy.13
  5.0 3.3 %copy.14 = bf16[4,2,128,16,128]{4,3,1,0,2:T(8,128)(2,1)} copy(bf16[4,2,128,16,128]{4,3,2,1,0:T(8,128)(2,1)S(1)} %bitcast.271) | data formatting | bytes 8388608 | tf_op jit(solution)/shard_map/reshape | solution.py:58
  8.3 13.9 %all-to-all-start = ((bf16[4,2,128,16,128]{4,3,1,0,2:T(8,128)(2,1)}), bf16[4,2,128,16,128]{4,3,1,0,2:T(8,128)(2,1)}, u32[]{:S(2)}, u32[]{:S(2)}) async-start(bf16[4,2,128,16,128]{4,3,1,0,2:T(8,128)(2,1)} %copy.14), calls=%async_computation | async-start | bytes 8388608 | tf_op jit(solution)/shard_map/all_to_all | solution.py:60
  22.7 91.9 %all-to-all-done = bf16[4,2,128,16,128]{4,3,1,0,2:T(8,128)(2,1)} async-done(((bf16[4,2,128,16,128]{4,3,1,0,2:T(8,128)(2,1)}), bf16[4,2,128,16,128]{4,3,1,0,2:T(8,128)(2,1)}, u32[]{:S(2)}, u32[]{:S(2)}) %all-to-all-start) | async-done | bytes 4194336 | tf_op jit(solution)/shard_map/all_to_all | solution.py:60
  114.6 4.1 %abs_reduce_fusion = bf16[4,2,128]{1,0,2:T(4,128)(2,1)S(1)} fusion(bf16[4,2,128,16,128]{4,3,1,0,2:T(8,128)(2,1)} %all-to-all-done), kind=kLoop, calls=%fused_computation.11 | loop fusion | flops 4193280 | bytes 4196352 | tf_op jit(solution)/shard_map/reduce_max | solution.py:63
  118.6 0.9 copy.18
  120.1 2.9 %copy.15 = bf16[4,2,128,16,128]{4,3,2,1,0:T(8,128)(2,1)S(1)} copy(bf16[4,2,128,16,128]{4,3,1,0,2:T(8,128)(2,1)} %all-to-all-done) | data formatting | bytes 8388608 | tf_op jit(solution)/shard_map/all_to_all | solution.py:60
  123.1 1.2 convert_bitcast_fusion
  124.3 1.0 copy.16
  125.3 2.7 %fusion.3 = bf16[4,2,2,1024,128]{4,3,2,1,0:T(8,128)(2,1)S(1)} fusion(f32[4,2,2,64,16,128]{5,4,3,2,1,0:T(8,128)S(1)} %copy.16, f32[4,2,2,1024]{3,2,1,0:T(2,128)S(1)} %div.30), kind=kLoop, calls=%fused_computation.10 | loop fusion | flops 4194304 | bytes 12648448 | tf_op jit(solution)/shard_map/convert_element_type | solution.py:65
  128.2 0.2 fusion.12
  128.4 1.6 %copy-done = bf16[4,2,2,1024,128]{4,3,2,1,0:T(8,128)(2,1)} copy-done((bf16[4,2,2,1024,128]{4,3,2,1,0:T(8,128)(2,1)}, bf16[4,2,2,1024,128]{4,3,2,1,0:T(8,128)(2,1)S(1)}, u32[]{:S(2)}) %copy-start) | copy-done | bytes 4194328
  130.0 0.2 fusion.13
  131.3 1.4 fusion.40
  132.6 1.4 fusion.36
  134.2 0.3 fusion.37
  134.8 0.3 fusion.8
  135.1 0.3 fusion.9
  135.4 0.3 fusion.10
  135.7 0.3 fusion.11
  136.1 10.6 %all-gather.1 = f32[4,66,128]{2,1,0:T(8,128)S(1)} all-gather(f32[1,66,128]{2,1,0:T(8,128)S(1)} %maximum_bitcast_fusion), channel_id=2, replica_groups=mesh['seq'=4,'blk'=64] {'seq'}, dimensions={0}, use_global_device_ids=true | all-gather | bytes 168960 | tf_op jit(solution)/shard_map/all_gather | solution.py:19
  147.1 0.4 while.14
  147.6 0.6 convert_element_type.68
  (74 shorter events, 3.5 us)
Async XLA Ops:
  8.3 13.9 %copy-start.4 = (s32[16]{0:T(128)S(1)}, s32[16]{0:T(128)}, u32[]{:S(2)}) copy-start(s32[16]{0:T(128)} %param.9) | copy-start | bytes 196
  8.3 14.0 %copy-start.1 = (bf16[4,2,1024]{2,1,0:T(2,128)(2,1)S(1)}, bf16[4,2,1024]{2,1,0:T(2,128)(2,1)}, u32[]{:S(2)}) copy-start(bf16[4,2,1024]{2,1,0:T(2,128)(2,1)} %param.7) | copy-start | bytes 49156
  8.3 14.1 %copy-start.3 = (bf16[4,2,2,128]{3,2,1,0:T(2,128)(2,1)S(1)}, bf16[4,2,2,128]{3,2,1,0:T(2,128)(2,1)}, u32[]{:S(2)}) copy-start(bf16[4,2,2,128]{3,2,1,0:T(2,128)(2,1)} %param.8) | copy-start | bytes 12292
  8.3 106.3 %all-to-all-start = ((bf16[4,2,128,16,128]{4,3,1,0,2:T(8,128)(2,1)}), bf16[4,2,128,16,128]{4,3,1,0,2:T(8,128)(2,1)}, u32[]{:S(2)}, u32[]{:S(2)}) async-start(bf16[4,2,128,16,128]{4,3,1,0,2:T(8,128)(2,1)} %copy.14), calls=%async_computation | async-start | bytes 8388608 | tf_op jit(solution)/shard_map/all_to_all | solution.py:60
  119.9 3.2 %copy-start.2 = (f32[4,2,2,8]{3,2,1,0:T(2,128)}, f32[4,2,2,8]{3,2,1,0:T(2,128)S(1)}, u32[]{:S(2)}) copy-start(f32[4,2,2,8]{3,2,1,0:T(2,128)S(1)} %copy.19) | copy-start | bytes 1540
  128.0 2.0 %copy-start = (bf16[4,2,2,1024,128]{4,3,2,1,0:T(8,128)(2,1)}, bf16[4,2,2,1024,128]{4,3,2,1,0:T(8,128)(2,1)S(1)}, u32[]{:S(2)}) copy-start(bf16[4,2,2,1024,128]{4,3,2,1,0:T(8,128)(2,1)S(1)} %fusion.3) | copy-start | bytes 12582916
where the time goes:
time: 149 us; the launch traced here: 148 us
  waiting for transfers between devices  91.9 us (62%)
  local copies, waits for them, and re-layouts  17.1 us (11%)
  starting transfers between devices  13.9 us (9%)
  blocking collectives  10.6 us (7%)
  other arithmetic  9.28 us (6%)
  matrix products  4.6 us (3%)
    all_to_all x1, waiting for transfers between devices, on_device(): lax.all_to_all(arranged, 'blk', split_axis=2, concat_axis=3, tiled=True)  91.9 us
    all_to_all x1, starting transfers between devices, on_device(): lax.all_to_all(arranged, 'blk', split_axis=2, concat_axis=3, tiled=True)  13.9 us
    all_gather x1, blocking collectives, gathered_once(): both, at, found = (lax.all_gather(jnp.concatenate(lines), axis), 0, {})  10.6 us
    unnamed x20, local copies, waits for them, and re-layouts  5.27 us
    reduce_max x2, other arithmetic, on_device(): jnp.max(jnp.abs(grouped), axis=(4, 5)).astype(jnp.float32)  4.16 us
    reshape x1, local copies, waits for them, and re-layouts, on_device(): arranged = arranged.reshape(layers, 2, heads * batch, local_rows, HEAD_DIM)  3.26 us
    dot_general x4, matrix products, on_device(): jnp.einsum('pgd,prd->pgr', grouped_queries[layer], quant[layer, 0], prefe...  3.22 us
  transfers between devices with their start and end apart: 1, of which 1 were waited for; matrix products, arithmetic and copies ran while one was open for 0% of the time, Pallas kernels for 0%

commit v1 on v0

--- a/solution.py
+++ b/solution.py
@@ -1,11 +1,95 @@
 import jax
 import jax.numpy as jnp
 from jax import lax
+from jax.experimental import pallas as pl
+from jax.experimental.pallas import tpu as pltpu
 from jax.sharding import PartitionSpec as P
 
 HEAD_DIM = 128
 QUERY_GROUP = 8
 BLOCK = 128
+
+
+MESH = pl.DeviceIdType.MESH
+Z, X, Y = 8, 4, 2
+LAYERS, ROWS = 4, 16
+
+
+def place():
+    index = lax.axis_index("blk")
+    return lax.div(index, X * Y), lax.rem(lax.div(index, Y), X), lax.rem(index, Y)
+
+
+def partner(dz, dx, dy):
+    z, x, y = place()
+    return lax.rem(z + dz, Z), lax.rem(x + dx, X), lax.rem(y + dy, Y)
+
+
+def exchange_kernel(cache_ref, out_ref, send_sem, recv_sem):
+    z, x, y = place()
+    me = (z * X + x) * Y + y
+
+    def each(visit):
+        def plane(p, carry):
+            dx, dy = lax.div(p, Y), lax.rem(p, Y)
+            for i in range(Z - 1):
+                visit(i // 2 + 1 if i % 2 == 0 else Z - (i + 1) // 2, dx, dy)
+            pl.when(p > 0)(lambda: visit(0, dx, dy))
+            return carry
+
+        lax.fori_loop(0, X * Y, plane, 0)
+
+    def piece(ref, layer, pz, px, py):
+        pair = 2 * (px * Y + py)
+        columns = pl.ds(pl.multiple_of(pz * HEAD_DIM, HEAD_DIM), HEAD_DIM)
+        return ref.at[pl.ds(layer, 1), :, pl.ds(pair, 2), :, columns]
+
+    def landing(layer):
+        rows = pl.ds(pl.multiple_of(me * ROWS, ROWS), ROWS)
+        return out_ref.at[pl.ds(layer, 1), :, :, rows, :]
+
+    barrier = pltpu.get_barrier_semaphore()
+
+    def greet(dz, dx, dy):
+        pz, px, py = partner(dz, dx, dy)
+        pl.semaphore_signal(
+            barrier, inc=1, device_id={"blk": (pz * X + px) * Y + py}, device_id_type=MESH
+        )
+
+    each(greet)
+    pl.semaphore_wait(barrier, Z * X * Y - 1)
+
+    def layer_sends(layer, carry):
+        def send(dz, dx, dy):
+            pz, px, py = partner(dz, dx, dy)
+            pltpu.make_async_remote_copy(
+                src_ref=piece(cache_ref, layer, pz, px, py),
+                dst_ref=landing(layer),
+                send_sem=send_sem,
+                recv_sem=recv_sem,
+                device_id={"blk": (pz * X + px) * Y + py},
+                device_id_type=MESH,
+            ).start()
+
+        each(send)
+        pltpu.make_async_copy(piece(cache_ref, layer, z, x, y), landing(layer), recv_sem).start()
+        return carry
+
+    lax.fori_loop(0, LAYERS, layer_sends, 0)
+    pltpu.make_async_copy(out_ref, out_ref, recv_sem).wait()
+    sent = out_ref.at[:, :, :, pl.ds(0, (Z * X * Y - 1) * ROWS), :]
+    pltpu.make_async_copy(sent, sent, send_sem).wait()
+
+
+def exchange(kv_cache):
+    return pl.pallas_call(
+        exchange_kernel,
+        out_shape=jax.ShapeDtypeStruct((LAYERS, 2, 2, Z * X * Y * ROWS, HEAD_DIM), kv_cache.dtype),
+        in_specs=[pl.BlockSpec(memory_space=pl.ANY)],
+        out_specs=pl.BlockSpec(memory_space=pl.ANY),
+        scratch_shapes=[pltpu.SemaphoreType.DMA, pltpu.SemaphoreType.DMA],
+        compiler_params=pltpu.CompilerParams(collective_id=0, has_side_effects=True),
+    )(kv_cache)
 
 
 def gathered_once(shard, axis):
@@ -52,12 +136,8 @@
     pairs_here = heads * batch // blk_count
     seq_rows = local_rows * blk_count
     blocks_here = seq_rows // BLOCK
-    arranged = kv_cache.reshape(layers, 2, batch, local_rows, heads, HEAD_DIM).transpose(
-        0, 1, 4, 2, 3, 5
-    )
-    arranged = arranged.reshape(layers, 2, heads * batch, local_rows, HEAD_DIM)
     pair_start = blk_place * pairs_here
-    moved = lax.all_to_all(arranged, "blk", split_axis=2, concat_axis=3, tiled=True)
+    moved = exchange(kv_cache)
     grouped = moved.reshape(layers, 2, pairs_here, blocks_here, BLOCK, HEAD_DIM)
     block_scale = (
         jnp.maximum(jnp.max(jnp.abs(grouped), axis=(4, 5)).astype(jnp.float32), 1.0) / 127.0

time: 149 us -> 127 us (0.85)
  Pallas kernels: 0 us -> 103 us
  waiting for transfers between devices: 91.9 us -> 0 us
  local copies, waits for them, and re-layouts: 17.1 us -> 2.67 us
  starting transfers between devices: 13.9 us -> 0 us
  matrix products: 4.6 us -> 2.48 us
  blocking collectives: 10.6 us -> 8.98 us
    pallas_call x0 -> x1, Pallas kernels: none -> 103 us  [exchange(): pl.pallas_call(exchange_kernel, out_shape=jax.ShapeDtypeStruct((LAYERS, 2...]
    all_to_all x1 -> x0, waiting for transfers between devices: 91.9 us -> none  [on_device(): lax.all_to_all(arranged, 'blk', split_axis=2, concat_axis=3, tiled=True)]
    all_to_all x1 -> x0, starting transfers between devices: 13.9 us -> none  [on_device(): lax.all_to_all(arranged, 'blk', split_axis=2, concat_axis=3, tiled=True)]
    unnamed x20 -> x17, local copies, waits for them, and re-layouts: 5.27 us -> 0.35 us
    reshape x1 -> x0, local copies, waits for them, and re-layouts: 3.26 us -> none  [on_device(): arranged = arranged.reshape(layers, 2, heads * batch, local_rows, HEAD_DIM)]
    all_to_all x1 -> x0, local copies, waits for them, and re-layouts: 2.95 us -> none  [on_device(): lax.all_to_all(arranged, 'blk', split_axis=2, concat_axis=3, tiled=True)]
    dot_general x4, matrix products: 3.22 us -> 1.16 us  [on_device(): jnp.einsum('pgd,prd->pgr', grouped_queries[layer], quant[layer, 0], prefe...]
    convert_element_type x1, other arithmetic: 2.73 us -> 4.41 us  [on_device(): (grouped.astype(jnp.float32) / block_scale[..., None, None]).astype(jnp.b...]
  transfers between devices with their start and end apart: 1 -> 0, of which waited for: 1 -> 0; matrix products, arithmetic and copies ran while one was open for 0% -> 0% of each run, Pallas kernels for 0% -> 0%
where the time goes in v1:
time: 127 us
  Pallas kernels  103 us (81%)
  other arithmetic  9.35 us (7%)
  blocking collectives  8.98 us (7%)
  local copies, waits for them, and re-layouts  2.67 us (2%)
  matrix products  2.48 us (2%)
    pallas_call x1, Pallas kernels, exchange(): pl.pallas_call(exchange_kernel, out_shape=jax.ShapeDtypeStruct((LAYERS, 2...  103 us
    all_gather x1, blocking collectives, gathered_once(): both, at, found = (lax.all_gather(jnp.concatenate(lines), axis), 0, {})  8.98 us
    convert_element_type x1, other arithmetic, on_device(): (grouped.astype(jnp.float32) / block_scale[..., None, None]).astype(jnp.b...  4.41 us
    reduce_max x2, other arithmetic, on_device(): jnp.max(jnp.abs(grouped), axis=(4, 5)).astype(jnp.float32)  3.68 us

profile of v1, /device:TPU:1, one launch (start us, length us, event | category | flops | bytes accessed | tf_op | source)
XLA Modules:
  0.0 127.1 jit_solution(10622362845387562777)
XLA Ops:
  0.6 0.7 tile.4
  1.5 102.6 %shard_map.67 = bf16[4,2,2,1024,128]{4,3,2,1,0:T(8,128)(2,1)} custom-call(bf16[4,2,16,16,1024]{4,3,2,1,0:T(8,128)(2,1)} %cache_ref.1), custom_call_target="tpu_custom_call" | custom-call | tf_op jit(solution)/shard_map/pallas_call | solution.py:85
  104.2 3.6 %abs_reduce_fusion = bf16[4,2,2,1024]{3,2,1,0:T(2,128)(2,1)S(1)} fusion(bf16[4,2,2,1024,128]{4,3,2,1,0:T(8,128)(2,1)} %shard_map.67), kind=kLoop, calls=%fused_computation.9 | loop fusion | flops 4177920 | bytes 4227072 | tf_op jit(solution)/shard_map/reduce_max | solution.py:143
  107.8 0.1 reduce_max.90
  108.1 4.4 %divide_convert_fusion = bf16[4,2,2,1024,128]{4,3,2,1,0:T(8,128)(2,1)S(1)} fusion(bf16[4,2,2,1024,128]{4,3,2,1,0:T(8,128)(2,1)} %shard_map.67, f32[4,2,2,1024]{3,2,1,0:T(2,128)S(1)} %div.30), kind=kLoop, calls=%fused_computation.8 | loop fusion | flops 6291456 | bytes 8454144 | tf_op jit(solution)/shard_map/convert_element_type | solution.py:145
  112.5 0.3 fusion.39
  112.9 0.2 fusion.11
  113.1 0.2 fusion.12
  113.3 0.4 fusion.35
  114.1 0.1 fusion.34
  114.3 0.1 fusion.99
  114.4 0.3 fusion.7
  114.7 0.3 fusion.36
  115.1 0.3 fusion.8
  115.4 0.3 fusion.9
  115.8 0.3 fusion.10
  116.3 9.0 %all-gather.1 = f32[4,66,128]{2,1,0:T(8,128)S(1)} all-gather(f32[1,66,128]{2,1,0:T(8,128)S(1)} %maximum_bitcast_fusion), channel_id=2, replica_groups=mesh['seq'=4,'blk'=64] {'seq'}, dimensions={0}, use_global_device_ids=true | all-gather | bytes 168960 | tf_op jit(solution)/shard_map/all_gather | solution.py:103
  125.7 0.4 while.14
  125.8 0.1 fusion.109
  125.9 0.1 fusion.109
  126.1 0.1 fusion.109
  126.2 0.1 fusion.81
  126.3 0.1 divide_convert_fusion.1
  126.4 0.6 convert_element_type.56
  (56 shorter events, 1.7 us)
Async XLA Ops:
  107.9 4.6 %copy-start.1 = (f32[4,2,2,8]{3,2,1,0:T(2,128)}, f32[4,2,2,8]{3,2,1,0:T(2,128)S(1)}, u32[]{:S(2)}) copy-start(f32[4,2,2,8]{3,2,1,0:T(2,128)S(1)} %maximum_multiply_fusion) | copy-start | bytes 1540
  108.0 4.4 %copy-start.2 = (bf16[4,2,1024]{2,1,0:T(2,128)(2,1)S(1)}, bf16[4,2,1024]{2,1,0:T(2,128)(2,1)}, u32[]{:S(2)}) copy-start(bf16[4,2,1024]{2,1,0:T(2,128)(2,1)} %param.7) | copy-start | bytes 49156
  112.5 2.2 %copy-start = (bf16[4,2,2,1024,128]{4,3,2,1,0:T(8,128)(2,1)}, bf16[4,2,2,1024,128]{4,3,2,1,0:T(8,128)(2,1)S(1)}, u32[]{:S(2)}) copy-start(bf16[4,2,2,1024,128]{4,3,2,1,0:T(8,128)(2,1)S(1)} %divide_convert_fusion) | copy-start | bytes 12582916
  114.3 11.9 %copy-start.3 = (bf16[4,2,2,128]{3,2,1,0:T(2,128)(2,1)S(1)}, bf16[4,2,2,128]{3,2,1,0:T(2,128)(2,1)}, u32[]{:S(2)}) copy-start(bf16[4,2,2,128]{3,2,1,0:T(2,128)(2,1)} %param.8) | copy-start | bytes 12292
